TPU v7x, 32 devices: a whole 2x2x4 slice. The times are simulated.
32 devices in a mesh: seq: 8 (over z, y), head: 4 (over x, core).
Axes of the slice: x: 2, y: 2, z: 4, core: 2. Of those that a mesh axis runs over, the one named last changes fastest.
Arguments:
- queries: bfloat16 [4096, 12288], P(('seq', 'head')), may hold values from -8 to 8
- latent: bfloat16 [4096, 512], P(('seq', 'head')), may hold values from -6 to 6
- rope_keys: bfloat16 [4096, 64], P(('seq', 'head')), may hold values from -8 to 8
- key_weight: bfloat16 [512, 8192], P('seq', 'head'), may hold values from -0.25 to 0.25
- value_weight: bfloat16 [512, 8192], P('seq', 'head'), may hold values from -0.25 to 0.25
- doc_lengths: int32 [32], replicated, may hold values from 1 to 254, as said below
Outputs:
- attended: bfloat16 [4096, 8192], P(('seq', 'head'))
Inputs may be any that keep to these rules, and one draw needn't show every extreme that they name: `doc_lengths`: the documents lie in order in the pack and their lengths sum to 4096; document 0 starts at position 0 and every other document d starts strictly inside positions d * 128 to (d + 1) * 128 - 1, excluding the first of these; one length is exactly 254.
All inputs are finite; a program needn't handle non-finite values.
Results may differ from a plain program's by a relative error of at most 0.0062.
Values may be sent and summed in bfloat16 or wider, within the bound.
A program may use at most 128 MiB of HBM per device.

v0:
```python
import math

import jax
import jax.numpy as jnp
from jax import lax
from jax.sharding import PartitionSpec as P

NOPE = 128
ROPE = 64
VDIM = 128


lowest_score = -1e30


def shifted(value, axis, steps):
    count = lax.axis_size(axis)
    first, last = (max(0, -steps), min(count, count - steps))
    return lax.ppermute(value, axis, [(source, source + steps) for source in range(first, last)])


def document_of(doc_lengths, first_place, count):
    starts = jnp.cumsum(doc_lengths) - doc_lengths
    places = first_place + jnp.arange(count, dtype=jnp.int32)
    started = (starts[None, :] <= places[:, None]).astype(jnp.int32)
    return jnp.sum(started, axis=1) - 1


def shards(queries, latent, rope_keys, key_weight, value_weight, doc_lengths):
    tok_rows = queries.shape[0]
    groups = lax.axis_size("head")
    group_rows = tok_rows * groups
    local_heads = key_weight.shape[1] // NOPE
    qk_width = NOPE + ROPE
    block_rows = min(512, group_rows)
    score_scale = 1.0 / math.sqrt(qk_width)
    group_latent, group_rope = (
        lax.all_gather(latent, "head", axis=0, tiled=True),
        lax.all_gather(rope_keys, "head", axis=0, tiled=True),
    )
    by_heads = queries.reshape(tok_rows, groups, local_heads * qk_width)
    my_queries = lax.all_to_all(by_heads, "head", split_axis=1, concat_axis=0, tiled=True)
    my_queries = my_queries.reshape(group_rows, local_heads, qk_width)
    earlier_latent, earlier_rope = shifted((group_latent, group_rope), "seq", 1)
    latent_rows = jnp.concatenate([earlier_latent, group_latent], axis=0)
    key_sums = jnp.dot(
        latent_rows,
        lax.all_gather(key_weight, "seq", axis=0, tiled=True),
        preferred_element_type=jnp.float32,
    )
    value_sums = jnp.dot(
        latent_rows,
        lax.all_gather(value_weight, "seq", axis=0, tiled=True),
        preferred_element_type=jnp.float32,
    )
    keys_all = key_sums.astype(jnp.bfloat16)
    values_all = value_sums.astype(jnp.bfloat16)
    rope_all = jnp.concatenate([earlier_rope, group_rope], axis=0)
    first_place = lax.axis_index("seq") * group_rows - group_rows
    key_docs = document_of(doc_lengths, first_place, 2 * group_rows)
    key_blocks = group_rows // block_rows + 1

    def one_block(q_index):
        q_start = q_index * block_rows
        q_block = lax.dynamic_slice_in_dim(my_queries, q_start, block_rows, 0)
        q_nope = q_block[:, :, :NOPE]
        q_rope = q_block[:, :, NOPE:]
        q_docs = lax.dynamic_slice_in_dim(key_docs, group_rows + q_start, block_rows, 0)
        q_places = group_rows + q_start + jnp.arange(block_rows, dtype=jnp.int32)

        def attend(state_now, k_start):
            row_peak, row_sum, weighted = state_now
            k_nope = lax.dynamic_slice_in_dim(keys_all, k_start, block_rows, 0).reshape(
                block_rows, local_heads, NOPE
            )
            k_rope = lax.dynamic_slice_in_dim(rope_all, k_start, block_rows, 0)
            k_values = lax.dynamic_slice_in_dim(values_all, k_start, block_rows, 0).reshape(
                block_rows, local_heads, VDIM
            )
            k_docs = lax.dynamic_slice_in_dim(key_docs, k_start, block_rows, 0)
            k_places = k_start + jnp.arange(block_rows, dtype=jnp.int32)
            scores = jnp.einsum("ihd,jhd->hij", q_nope, k_nope, preferred_element_type=jnp.float32)
            scores = (
                scores
                + jnp.einsum("ihd,jd->hij", q_rope, k_rope, preferred_element_type=jnp.float32)
            ) * score_scale
            allowed = (q_docs[:, None] == k_docs[None, :]) & (
                k_places[None, :] <= q_places[:, None]
            )
            scores = jnp.where(allowed[None, :, :], scores, -jnp.inf)
            new_peak = jnp.maximum(row_peak, jnp.max(scores, axis=2))
            expo = jnp.exp(scores - new_peak[:, :, None])
            rescale = jnp.exp(row_peak - new_peak)
            row_sum = row_sum * rescale + jnp.sum(expo, axis=2)
            rounded = expo.astype(jnp.bfloat16)
            weighted = weighted * jnp.transpose(rescale)[:, :, None] + jnp.einsum(
                "hij,jhd->ihd", rounded, k_values, preferred_element_type=jnp.float32
            )
            return (new_peak, row_sum, weighted)

        def visit(k_index, state_now):
            k_start = (q_index + k_index) * block_rows
            return attend(state_now, k_start)

        start_state = (
            jnp.full((local_heads, block_rows), lowest_score, jnp.float32),
            jnp.zeros((local_heads, block_rows), jnp.float32),
            jnp.zeros((block_rows, local_heads, VDIM), jnp.float32),
        )
        row_peak, row_sum, weighted = lax.fori_loop(0, key_blocks, visit, start_state)
        mixed = weighted / jnp.transpose(row_sum)[:, :, None]
        return mixed.reshape(block_rows, local_heads * VDIM).astype(jnp.bfloat16)

    attended = lax.map(one_block, jnp.arange(group_rows // block_rows, dtype=jnp.int32))
    attended = attended.reshape(group_rows, local_heads * VDIM)
    return lax.all_to_all(attended, "head", split_axis=0, concat_axis=1, tiled=True)


def solution(mesh):
    placed = (
        P(("seq", "head"), None),
        P(("seq", "head"), None),
        P(("seq", "head"), None),
        P("seq", "head"),
        P("seq", "head"),
        P(),
    )
    return jax.shard_map(
        shards, mesh=mesh, in_specs=placed, out_specs=P(("seq", "head"), None), check_vma=False
    )
```

profile of v0, /device:TPU:24, one launch (start us, length us, event | category | flops | bytes accessed | tf_op | source)
XLA Modules:
  0.0 263.6 jit_solution(16397362102744043481)
XLA Ops:
  6.5 0.0 all-gather.5.cloned.1.call-start
  6.5 0.7 all-gather.5.cloned.1.call-update
  7.3 0.0 all-gather.3.cloned.1.call-start
  7.3 0.7 all-gather.3.cloned.1.call-update
  8.0 4.7 %copy.43 = bf16[128,12288]{0,1:T(8,128)(2,1)} copy(bf16[128,12288]{1,0:T(8,128)(2,1)} %param.8) | data formatting | bytes 6291456 | tf_op args[0]
  12.7 0.0 copy-start
  12.7 0.0 copy-start.1
  12.7 0.0 copy-start.2
  12.7 3.8 %all-to-all-start = ((bf16[128,4,3072]{0,2,1:T(8,128)(2,1)}), bf16[128,4,3072]{0,2,1:T(8,128)(2,1)S(1)}, u32[]{:S(2)}, u32[]{:S(2)}) async-start(bf16[128,4,3072]{0,2,1:T(8,128)(2,1)} %bitcast.61), calls=%async_computation | async-start | bytes 6291456 | tf_op jit(solution)/shard_map/all_to_all | solution.py:42
  16.5 0.0 copy-done
  16.5 41.0 %all_gather.12 = bf16[512,512]{1,0:T(8,128)(2,1)} all-gather(bf16[128,512]{1,0:T(8,128)(2,1)S(1)} %copy-done), channel_id=1, replica_groups=mesh['seq'=8,'head'=4] {'head'}, dimensions={0}, use_global_device_ids=true | all-gather | bytes 655360 | tf_op jit(solution)/shard_map/all_gather | solution.py:38
  57.5 3.4 %collective-permute-start = (bf16[512,512]{1,0:T(8,128)(2,1)}, bf16[512,512]{1,0:T(8,128)(2,1)}, u32[]{:S(2)}, u32[]{:S(2)}) collective-permute-start(bf16[512,512]{1,0:T(8,128)(2,1)} %all_gather.12), channel_id=1, source_target_pairs={{0,4},{4,8},{8,12},{12,16},{16,20},{20,24},{24,28},{1,5},{5,9},{9,... | collective-permute-start | bytes 1572872 | tf_op jit(solution)/shard_map/ppermute | solution.py:19
  60.9 0.0 copy-done.1
  60.9 5.3 %all_gather.14 = bf16[512,64]{0,1:T(8,128)(2,1)S(1)} all-gather(bf16[128,64]{0,1:T(8,128)(2,1)S(1)} %copy-done.1), channel_id=1, replica_groups=mesh['seq'=8,'head'=4] {'head'}, dimensions={0}, use_global_device_ids=true | all-gather | bytes 81920 | tf_op jit(solution)/shard_map/all_gather | solution.py:39
  66.2 1.9 collective-permute-start.1
  68.1 0.0 copy-done.2
  68.1 0.1 copy.42
  68.2 0.1 reduce-window.9
  68.3 0.1 reduce
  68.4 0.1 convert_reduce_fusion
  68.6 15.9 %collective-permute-done.1 = bf16[512,64]{0,1:T(8,128)(2,1)S(1)} collective-permute-done((bf16[512,64]{0,1:T(8,128)(2,1)S(1)}, bf16[512,64]{0,1:T(8,128)(2,1)S(1)}, u32[]{:S(2)}, u32[]{:S(2)}) %collective-permute-start.1) | collective-permute-done | bytes 65568 | tf_op jit(solution)/shard_map/ppermute | solution.py:19
  84.5 0.0 collective-permute-done
  84.5 1.9 constant_dynamic-update-slice_fusion.1
  86.4 1.9 constant_dynamic-update-slice_fusion
  88.3 0.0 all-to-all-done
  88.3 15.6 %copy.44 = bf16[4,128,1,3072]{1,0,3,2:T(4,128)(2,1)} copy(bf16[4,128,1,3072]{1,3,0,2:T(8,128)(2,1)S(1)} %bitcast.60) | data formatting | bytes 6291456 | tf_op jit(solution)/shard_map/all_to_all | solution.py:42
  103.9 4.0 %reshape.132 = bf16[512,16,192]{0,2,1:T(8,128)(2,1)S(1)} reshape(bf16[4,128,1,3072]{1,0,3,2:T(4,128)(2,1)} %copy.44) | data formatting | bytes 6291456 | tf_op jit(solution)/shard_map/reshape | solution.py:43
  107.9 1.5 slice.11
  109.4 1.1 slice.12
  110.5 3.9 %copy.46 = bf16[512,16,128]{2,0,1:T(8,128)(2,1)} copy(bf16[512,16,128]{0,2,1:T(8,128)(2,1)} %slice.11) | data formatting | bytes 4194304
  114.4 0.0 all-gather.5.cloned.1.call-done
  114.4 6.2 %convolution_convert_fusion = bf16[1024,2048]{1,0:T(8,128)(2,1)} fusion(bf16[1024,512]{1,0:T(8,128)(2,1)} %constant_dynamic-update-slice_fusion, bf16[512,2048]{1,0:T(8,128)(2,1)} %all-gather.5.cloned.1.call-done), kind=kOutput, calls=%fused_computation.25 | convolution fusion | flops 2149580800 | bytes 7340032 | tf_op jit(solution)/shard_map/dot_general | solution.py:51
  120.6 0.0 all-gather.3.cloned.1.call-done
  120.6 6.2 %convolution_convert_fusion.1 = bf16[1024,2048]{1,0:T(8,128)(2,1)} fusion(bf16[1024,512]{1,0:T(8,128)(2,1)} %constant_dynamic-update-slice_fusion, bf16[512,2048]{1,0:T(8,128)(2,1)} %all-gather.3.cloned.1.call-done), kind=kOutput, calls=%fused_computation.26 | convolution fusion | flops 2149580800 | bytes 7340032 | tf_op jit(solution)/shard_map/dot_general | solution.py:46
  126.8 87.3 %while.27 = (s32[]{:T(128)}, f32[16,512]{1,0:T(8,128)S(1)}, f32[16,512]{1,0:T(8,128)S(1)}, f32[512,16,128]{0,2,1:T(8,128)}, s32[512]{0:T(512)S(1)}, /*index=5*/s...) while((s32[]{:T(128)}, f32[16,512]{1,0:T(8,128)S(1)}, ...), condition=%wide.region_5.6_spmd.clone, body=%wide.region_2.5_spmd.clone.sunk | while | flops 2721891328 | bytes 117522640 | solution.py:110
  126.8 0.1 dynamic_slice.63
  126.9 0.3 compare_and_fusion.2
  127.2 4.8 %constant_dynamic-slice_fusion.3 = (bf16[512,2048]{1,0:T(8,128)(2,1)}, bf16[512,2048]{1,0:T(8,128)(2,1)}) fusion(bf16[1024,2048]{1,0:T(8,128)(2,1)} %get-tuple-element.540, s32[]{:T(128)S(6)} %select_n.30, bf16[1024,2048]{1,0:T(8,128)(2,1)} %get-tuple-element.536), kind=kLoop, calls=%fused_computation.21.clone.1 | loop fusion | bytes 8388612 | tf_op jit(solution)/shard_map/while/body/eval_jaxpr/while/body/eval_jaxpr/dynamic_slice | solution.py:77
  132.1 2.9 %copy.58 = bf16[512,2048]{0,1:T(8,128)(2,1)S(1)} copy(bf16[512,2048]{1,0:T(8,128)(2,1)} %get-tuple-element.492) | data formatting | bytes 4194304 | tf_op jit(solution)/shard_map/while/body/eval_jaxpr/while/body/eval_jaxpr/dynamic_slice | solution.py:73
  134.9 4.0 %fusion.41 = f32[16,512,512]{2,1,0:T(8,128)S(1)} fusion(bf16[512,16,128]{0,2,1:T(8,128)(2,1)S(1)} %bitcast.59, bf16[512,16,128]{2,0,1:T(8,128)(2,1)} %get-tuple-element.537), kind=kOutput, calls=%fused_computation.34.clone.1 | convolution fusion | flops 1073741824 | bytes 20971520 | tf_op jit(solution)/shard_map/while/body/eval_jaxpr/while/body/eval_jaxpr/ihd,jhd->hij/dot_general | solution.py:82
  138.9 9.0 %fusion.42 = (f32[16,512]{1,0:T(8,128)S(1)}, f32[16,512,512]{1,2,0:T(8,128)}) fusion(bf16[512,16,64]{0,2,1:T(8,128)(2,1)} %get-tuple-element.539, bf16[1024,64]{0,1:T(8,128)(2,1)S(1)} %get-tuple-element.538, s32[]{:T(128)S(6)} %select_n.30, f32[16,512,512]{2,1,0:T(8,128)S(1)} %fusion.41, pred[512,512]{0,1:T(8,128)(4,1)S(1)} %compare_and_fusion.2), kind=kOutput, calls=%fused_computation.33.clone.1 | convolution fusion | flops 553639936 | bytes 34963460 | tf_op jit(solution)/shard_map/while/body/eval_jaxpr/while/body/eval_jaxpr/ihd,jd->hij/dot_general | solution.py:85
  147.9 2.9 %copy.59 = bf16[512,2048]{0,1:T(8,128)(2,1)S(1)} copy(bf16[512,2048]{1,0:T(8,128)(2,1)} %get-tuple-element.498) | data formatting | bytes 4194304 | tf_op jit(solution)/shard_map/while/body/eval_jaxpr/while/body/eval_jaxpr/dynamic_slice | solution.py:77
  150.8 10.8 %bitcast_add_fusion.3 = f32[512,16,128]{0,2,1:T(8,128)} fusion(f32[512,16,128]{0,2,1:T(8,128)} %get-tuple-element.518, bf16[512,16,128]{0,2,1:T(8,128)(2,1)S(1)} %bitcast.58, f32[16,512,512]{1,2,0:T(8,128)} %get-tuple-element.497, f32[16,512]{1,0:T(8,128)S(1)} %get-tuple-element.531, f32[512,16]{0,1:T(8,128)S(1)} %get-tuple-element.499, pred[]{:T(512)S(6)} %compare.3), kind=kOutput, calls=%fused_computation.9.clone.1 | convolution fusion | flops 1085276160 | bytes 27328512 | tf_op jit(solution)/shard_map/while/body/eval_jaxpr/while/body/eval_jaxpr/hij,jhd->ihd/dot_general | solution.py:96
  161.6 8.3 %fusion.44 = f32[16,512]{1,0:T(8,128)S(1)} fusion(f32[16,512,512]{1,2,0:T(8,128)} %get-tuple-element.497, f32[16,512]{1,0:T(8,128)S(1)} %get-tuple-element.531), kind=kLoop, calls=%fused_computation.6.clone.1 | loop fusion | flops 8380416 | bytes 16842752 | tf_op jit(solution)/shard_map/while/body/eval_jaxpr/while/body/eval_jaxpr/reduce_sum | solution.py:94
  169.9 0.1 dynamic_slice.63
  170.0 0.3 compare_and_fusion.2
  170.3 4.8 %constant_dynamic-slice_fusion.3 = (bf16[512,2048]{1,0:T(8,128)(2,1)}, bf16[512,2048]{1,0:T(8,128)(2,1)}) fusion(bf16[1024,2048]{1,0:T(8,128)(2,1)} %get-tuple-element.540, s32[]{:T(128)S(6)} %select_n.30, bf16[1024,2048]{1,0:T(8,128)(2,1)} %get-tuple-element.536), kind=kLoop, calls=%fused_computation.21.clone.1 | loop fusion | bytes 8388612 | tf_op jit(solution)/shard_map/while/body/eval_jaxpr/while/body/eval_jaxpr/dynamic_slice | solution.py:77
  175.1 2.9 %copy.58 = bf16[512,2048]{0,1:T(8,128)(2,1)S(1)} copy(bf16[512,2048]{1,0:T(8,128)(2,1)} %get-tuple-element.492) | data formatting | bytes 4194304 | tf_op jit(solution)/shard_map/while/body/eval_jaxpr/while/body/eval_jaxpr/dynamic_slice | solution.py:73
  178.0 4.0 %fusion.41 = f32[16,512,512]{2,1,0:T(8,128)S(1)} fusion(bf16[512,16,128]{0,2,1:T(8,128)(2,1)S(1)} %bitcast.59, bf16[512,16,128]{2,0,1:T(8,128)(2,1)} %get-tuple-element.537), kind=kOutput, calls=%fused_computation.34.clone.1 | convolution fusion | flops 1073741824 | bytes 20971520 | tf_op jit(solution)/shard_map/while/body/eval_jaxpr/while/body/eval_jaxpr/ihd,jhd->hij/dot_general | solution.py:82
  182.0 9.0 %fusion.42 = (f32[16,512]{1,0:T(8,128)S(1)}, f32[16,512,512]{1,2,0:T(8,128)}) fusion(bf16[512,16,64]{0,2,1:T(8,128)(2,1)} %get-tuple-element.539, bf16[1024,64]{0,1:T(8,128)(2,1)S(1)} %get-tuple-element.538, s32[]{:T(128)S(6)} %select_n.30, f32[16,512,512]{2,1,0:T(8,128)S(1)} %fusion.41, pred[512,512]{0,1:T(8,128)(4,1)S(1)} %compare_and_fusion.2), kind=kOutput, calls=%fused_computation.33.clone.1 | convolution fusion | flops 553639936 | bytes 34963460 | tf_op jit(solution)/shard_map/while/body/eval_jaxpr/while/body/eval_jaxpr/ihd,jd->hij/dot_general | solution.py:85
  190.9 2.9 %copy.59 = bf16[512,2048]{0,1:T(8,128)(2,1)S(1)} copy(bf16[512,2048]{1,0:T(8,128)(2,1)} %get-tuple-element.498) | data formatting | bytes 4194304 | tf_op jit(solution)/shard_map/while/body/eval_jaxpr/while/body/eval_jaxpr/dynamic_slice | solution.py:77
  193.8 12.0 %bitcast_add_fusion.3 = f32[512,16,128]{0,2,1:T(8,128)} fusion(f32[512,16,128]{0,2,1:T(8,128)} %get-tuple-element.518, bf16[512,16,128]{0,2,1:T(8,128)(2,1)S(1)} %bitcast.58, f32[16,512,512]{1,2,0:T(8,128)} %get-tuple-element.497, f32[16,512]{1,0:T(8,128)S(1)} %get-tuple-element.531, f32[512,16]{0,1:T(8,128)S(1)} %get-tuple-element.499, pred[]{:T(512)S(6)} %compare.3), kind=kOutput, calls=%fused_computation.9.clone.1 | convolution fusion | flops 1085276160 | bytes 27328512 | tf_op jit(solution)/shard_map/while/body/eval_jaxpr/while/body/eval_jaxpr/hij,jhd->ihd/dot_general | solution.py:96
  205.8 8.3 %fusion.44 = f32[16,512]{1,0:T(8,128)S(1)} fusion(f32[16,512,512]{1,2,0:T(8,128)} %get-tuple-element.497, f32[16,512]{1,0:T(8,128)S(1)} %get-tuple-element.531), kind=kLoop, calls=%fused_computation.6.clone.1 | loop fusion | flops 8380416 | bytes 16842752 | tf_op jit(solution)/shard_map/while/body/eval_jaxpr/while/body/eval_jaxpr/reduce_sum | solution.py:94
  214.1 2.8 %divide_convert_fusion = bf16[512,16,128]{0,2,1:T(8,128)(2,1)S(1)} fusion(f32[512,16,128]{0,2,1:T(8,128)} %get-tuple-element.292, f32[512,16]{0,1:T(8,128)S(1)} %bitcast.63), kind=kLoop, calls=%fused_computation.24 | loop fusion | flops 2097152 | bytes 6324224 | tf_op jit(solution)/shard_map/while/body/eval_jaxpr/convert_element_type | solution.py:112
  216.9 2.0 reshape.136
  219.0 3.0 %copy.53 = bf16[4,128,2048]{2,1,0:T(8,128)(2,1)S(1)} copy(bf16[4,128,2048]{1,0,2:T(4,128)(2,1)} %reshape.136) | data formatting | bytes 4194304 | tf_op jit(solution)/shard_map/while/body/eval_jaxpr/convert_element_type | solution.py:112
  221.9 28.9 %all_to_all.31 = bf16[4,128,2048]{2,1,0:T(8,128)(2,1)} all-to-all(bf16[4,128,2048]{2,1,0:T(8,128)(2,1)S(1)} %copy.53), channel_id=1, replica_groups=mesh['seq'=8,'head'=4] {'head'}, dimensions={0} | all-to-all | bytes 4194304 | tf_op jit(solution)/shard_map/all_to_all | solution.py:116
  250.8 3.0 %copy.49 = bf16[4,128,2048]{1,2,0:T(8,128)(2,1)S(1)} copy(bf16[4,128,2048]{2,1,0:T(8,128)(2,1)} %all_to_all.31) | data formatting | bytes 4194304 | tf_op jit(solution)/shard_map/all_to_all | solution.py:116
  253.9 2.9 %copy.50 = bf16[128,8192]{1,0:T(8,128)(2,1)} copy(bf16[128,8192]{0,1:T(8,128)(2,1)S(1)} %bitcast.62) | data formatting | bytes 4194304 | tf_op jit(solution)/shard_map/all_to_all | solution.py:116
  (16 shorter events, 0.1 us)
Async XLA Ops:
  6.5 107.9 %all-gather.5.cloned.1.call-start = ((), (), s32[]{:S(2)}) async-start(), calls=%async_computation.3 | async-start | bytes 2359296 | tf_op jit(solution)/shard_map/all_gather | solution.py:53
  7.3 113.4 %all-gather.3.cloned.1.call-start = ((), (), s32[]{:S(2)}) async-start(), calls=%async_computation.2 | async-start | bytes 2359296 | tf_op jit(solution)/shard_map/all_gather | solution.py:48
  12.7 3.9 %copy-start = (bf16[128,512]{1,0:T(8,128)(2,1)S(1)}, bf16[128,512]{1,0:T(8,128)(2,1)}, u32[]{:S(2)}) copy-start(bf16[128,512]{1,0:T(8,128)(2,1)} %param.9) | copy-start | bytes 393220
  12.7 48.3 %copy-start.1 = (bf16[128,64]{0,1:T(8,128)(2,1)S(1)}, bf16[128,64]{0,1:T(8,128)(2,1)}, u32[]{:S(2)}) copy-start(bf16[128,64]{0,1:T(8,128)(2,1)} %param.10) | copy-start | bytes 49156
  12.7 55.5 %copy-start.2 = (s32[32]{0:T(128)S(1)}, s32[32]{0:T(128)}, u32[]{:S(2)}) copy-start(s32[32]{0:T(128)} %param.13) | copy-start | bytes 388
  12.7 75.6 %all-to-all-start = ((bf16[128,4,3072]{0,2,1:T(8,128)(2,1)}), bf16[128,4,3072]{0,2,1:T(8,128)(2,1)S(1)}, u32[]{:S(2)}, u32[]{:S(2)}) async-start(bf16[128,4,3072]{0,2,1:T(8,128)(2,1)} %bitcast.61), calls=%async_computation | async-start | bytes 6291456 | tf_op jit(solution)/shard_map/all_to_all | solution.py:42
  57.5 27.0 %collective-permute-start = (bf16[512,512]{1,0:T(8,128)(2,1)}, bf16[512,512]{1,0:T(8,128)(2,1)}, u32[]{:S(2)}, u32[]{:S(2)}) collective-permute-start(bf16[512,512]{1,0:T(8,128)(2,1)} %all_gather.12), channel_id=1, source_target_pairs={{0,4},{4,8},{8,12},{12,16},{16,20},{20,24},{24,28},{1,5},{5,9},{9,... | collective-permute-start | bytes 1572872 | tf_op jit(solution)/shard_map/ppermute | solution.py:19
  66.2 18.3 %collective-permute-start.1 = (bf16[512,64]{0,1:T(8,128)(2,1)S(1)}, bf16[512,64]{0,1:T(8,128)(2,1)S(1)}, u32[]{:S(2)}, u32[]{:S(2)}) collective-permute-start(bf16[512,64]{0,1:T(8,128)(2,1)S(1)} %all_gather.14), channel_id=1, source_target_pairs={{0,4},{4,8},{8,12},{12,16},{16,20},{20,24},{24,28},{1,5},{5,9},{9,... | collective-permute-start | bytes 196616 | tf_op jit(solution)/shard_map/ppermute | solution.py:19
Sparse Core Ops, SparseCore 0:
  9.5 48.5 all-gather.4
  60.2 50.0 all-gather.2
where the time goes:
time: 265 us; the launch traced here: 264 us
  blocking collectives  75.1 us (28%)
  local copies, waits for them, and re-layouts  66.8 us (25%)
  matrix products  61.1 us (23%)
  other arithmetic  20.3 us (8%)
  waiting for transfers between devices  17.4 us (7%)
  between operations  13.6 us (5%)
  starting transfers between devices  9.2 us (3%)
    all_gather x1, blocking collectives, shards(): lax.all_gather(latent, 'head', axis=0, tiled=True)  41 us
    all_to_all x1, blocking collectives, shards(): lax.all_to_all(attended, 'head', split_axis=0, concat_axis=1, tiled=True)  28.9 us
    dot_general x2, matrix products, attend(): jnp.einsum('hij,jhd->ihd', rounded, k_values, preferred_element_type=jnp....  22.8 us
    dot_general x2, matrix products, attend(): jnp.einsum('ihd,jd->hij', q_rope, k_rope, preferred_element_type=jnp.floa...  18 us
    reduce_sum x2, other arithmetic, attend(): row_sum = row_sum * rescale + jnp.sum(expo, axis=2)  16.5 us
    ppermute x2, waiting for transfers between devices, shifted(): lax.ppermute(value, axis, [(source, source + steps) for source in range(f...  15.9 us
    all_to_all x1, local copies, waits for them, and re-layouts, shards(): lax.all_to_all(by_heads, 'head', split_axis=1, concat_axis=0, tiled=True)  15.6 us
    dynamic_slice x4, local copies, waits for them, and re-layouts, attend(): lax.dynamic_slice_in_dim(values_all, k_start, block_rows, 0)  15.4 us
  transfers between devices with their start and end apart: 5, of which 1 were waited for; matrix products, arithmetic and copies ran while one was open for 16% of the time, Pallas kernels for 0%

commit v1 on v0

v1 whole, which is shorter than its diff:
```python
import functools
import math

import jax
import jax.numpy as jnp
from jax import lax
from jax.experimental import pallas as pl
from jax.experimental.pallas import tpu as pltpu
from jax.sharding import PartitionSpec as P

NOPE = 128
ROPE = 64
VDIM = 128
QK = NOPE + ROPE
LOG2E = 1.4426950408889634

MESH = pl.DeviceIdType.MESH


def kernel(
    sizes, queries, latrope, key_weight, value_weight, lengths, out,
    lat_all, wk, wv, qbuf, kaug, vbuf, bias, obuf,
    lat_sem, lat_send, mate_send, q_sem, q_send, w_own, w_recv, w_send, o_sem, o_send,
):
    n_seq, n_head, look, chunks, chunk_heads = sizes
    tok, rank = latrope.shape[0], latrope.shape[1] - 2 * ROPE
    rows = key_weight.shape[0]
    half = n_seq // 2
    xs = n_head // 2
    slots = look + n_head
    span = (look + 1) * tok
    cw = chunk_heads * NOPE
    qw = chunk_heads * QK
    seq, head = lax.axis_index("seq"), lax.axis_index("head")
    core, x = head % 2, head // 2
    mate = head + 1 - 2 * core

    odd = seq % 2
    place = (seq // 2) * (1 - odd) + (n_seq - 1 - seq // 2) * odd

    def at_place(where):
        where = (where + n_seq) % n_seq
        fold = where // half
        return 2 * where * (1 - fold) + (2 * (n_seq - 1 - where) + 1) * fold

    after, before = at_place(place + 1), at_place(place - 1)
    next_seq, last_seq = (seq + 1) % n_seq, (seq + n_seq - 1) % n_seq

    barrier = pltpu.get_barrier_semaphore()

    def greet(to_seq, to_head):
        pl.semaphore_signal(barrier, inc=1, device_id=(to_seq, to_head), device_id_type=MESH)

    for k in range(1, n_head):
        greet(seq, (head + k) % n_head)
    greet(after, head)
    greet(before, head)
    for k in range(xs):
        greet(next_seq, ((x + k) % xs) * 2 + core)
        greet(last_seq, ((x + k) % xs) * 2 + core)

    def own_copies():
        pltpu.make_async_copy(latrope, lat_all.at[look + head], lat_sem.at[look + head]).start()
        for c in range(chunks):
            pltpu.make_async_copy(
                queries.at[:, pl.ds(pl.multiple_of(head * chunks * qw + c * qw, 128), qw)],
                qbuf.at[c, head], q_sem.at[c, head],
            ).start()
            for kv, (source, held) in enumerate(((key_weight, wk), (value_weight, wv))):
                pltpu.make_async_copy(
                    source.at[:, pl.ds(c * cw, cw)], held.at[c, seq], w_own.at[c, kv]
                ).start()

    own_copies()
    pl.semaphore_wait(barrier, n_head - 1 + 2 + 2 * xs)

    def lat_copy(k, to_seq, slot):
        return pltpu.make_async_remote_copy(
            src_ref=latrope, dst_ref=lat_all.at[slot],
            send_sem=lat_send.at[k], recv_sem=lat_sem.at[slot],
            device_id=(to_seq, ((x + k % xs) % xs) * 2 + core), device_id_type=MESH,
        )

    def ring_parts(t):
        both = [(0, 0), (0, 1), (1, 0), (1, 1)]
        return both if t < half else [(0, 0), (1, 1)]

    def ring_copy(c, t, way, kv):
        origin = at_place(place - (t - 1)) if way == 0 else at_place(place + (t - 1))
        source, held = ((key_weight, wk), (value_weight, wv))[kv]
        src = source.at[:, pl.ds(c * cw, cw)] if t == 1 else held.at[c, origin]
        index = t - 1
        return pltpu.make_async_remote_copy(
            src_ref=src, dst_ref=held.at[c, origin],
            send_sem=w_send.at[c, index, way, kv], recv_sem=w_recv.at[c, index, way, kv],
            device_id=(after if way == 0 else before, head), device_id_type=MESH,
        )

    def ring_start(c, t):
        for way, kv in ring_parts(t):
            ring_copy(c, t, way, kv).start()

    def ring_take(c, t):
        for way, kv in ring_parts(t):
            origin = at_place(place - t) if way == 0 else at_place(place + t)
            landed = (wk, wv)[kv].at[c, origin]
            pltpu.make_async_copy(landed, landed, w_recv.at[c, t - 1, way, kv]).wait()
            if t + 1 <= half and (way, kv) in ring_parts(t + 1):
                ring_copy(c, t + 1, way, kv).start()

    def q_copy(c, k):
        peer = (head + k) % n_head
        return pltpu.make_async_remote_copy(
            src_ref=queries.at[:, pl.ds(pl.multiple_of(peer * chunks * qw + c * qw, 128), qw)],
            dst_ref=qbuf.at[c, head],
            send_sem=q_send.at[c, k - 1], recv_sem=q_sem.at[c, head],
            device_id=(seq, peer), device_id_type=MESH,
        )

    def o_copy(c, k):
        peer = (head + k) % n_head
        return pltpu.make_async_remote_copy(
            src_ref=obuf.at[c, peer],
            dst_ref=out.at[:, pl.ds(pl.multiple_of(head * chunks * cw + c * cw, 128), cw)],
            send_sem=o_send.at[c, k - 1], recv_sem=o_sem.at[c, head],
            device_id=(seq, peer), device_id_type=MESH,
        )

    def o_own(c):
        return pltpu.make_async_copy(
            obuf.at[c, head],
            out.at[:, pl.ds(pl.multiple_of(head * chunks * cw + c * cw, 128), cw)],
            o_sem.at[c, head],
        )

    for k in range(1, xs):
        lat_copy(k, seq, look + head).start()

    @pl.when(head >= n_head - look)
    def _():
        for k in range(xs):
            lat_copy(xs + k, next_seq, head - (n_head - look)).start()

    for c in range(min(2, chunks)):
        ring_start(c, 1)
    for c in range(chunks):
        for k in range(1, n_head):
            q_copy(c, k).start()

    docs = lengths.shape[0]
    later = lax.broadcasted_iota(jnp.int32, (docs, docs), 1)
    earlier = lax.broadcasted_iota(jnp.int32, (docs, docs), 0)
    starts = jnp.sum(jnp.where(earlier < later, lengths[...], 0), axis=0, keepdims=True)
    first = seq * n_head * tok

    def mask_tile(j, carry):
        q_place = first + j * tok + lax.broadcasted_iota(jnp.int32, (tok, 1), 0)
        begun = jnp.max(jnp.where(starts <= q_place, starts, 0), axis=1, keepdims=True)
        k_place = first + (j - look) * tok + lax.broadcasted_iota(jnp.int32, (tok, span), 1)
        seen = (k_place >= begun) & (k_place <= q_place)
        bias[j] = jnp.where(seen, 0.0, -jnp.inf)
        return carry

    lax.fori_loop(0, n_head, mask_tile, 0)

    def lat_wait(slot):
        pltpu.make_async_copy(lat_all.at[slot], lat_all.at[slot], lat_sem.at[slot]).wait()

    def mate_copy(i):
        slot = 2 * i + core
        return pltpu.make_async_remote_copy(
            src_ref=lat_all.at[slot], dst_ref=lat_all.at[slot],
            send_sem=mate_send.at[i], recv_sem=lat_sem.at[slot],
            device_id=(seq, mate), device_id_type=MESH,
        )

    def lat_all_in():
        for i in list(range(look // 2, slots // 2)) + list(range(look // 2)):
            lat_wait(2 * i + core)
            mate_copy(i).start()
        for i in range(slots // 2):
            lat_wait(2 * i + 1 - core)

    def rope_in():
        lane = lax.broadcasted_iota(jnp.int32, (tok, 2 * ROPE), 1)
        del lane

        def fill(slot, carry):
            tail = lat_all[slot, :, rank:]
            rolled = pltpu.roll(tail.astype(jnp.float32), ROPE, axis=1).astype(jnp.bfloat16)
            at = pl.ds(pl.multiple_of(slot * tok, tok), tok)
            for h in range(chunk_heads):
                kaug[h, at, NOPE:] = tail if h % 2 == 0 else rolled
            return carry

        lax.fori_loop(0, slots, fill, 0)

    block = slots * tok // 2

    def project(c):
        for kv in range(2):
            mine = (wk, wv)[kv].at[c, seq]
            pltpu.make_async_copy(mine, mine, w_own.at[c, kv]).wait()

        def rows_of(i, carry):
            at = pl.ds(pl.multiple_of(i * block, block), block)
            lat = lat_all[pl.ds(i * (slots // 2), slots // 2), :, :rank].reshape(block, rank)
            low = lax.broadcasted_iota(jnp.int32, (block, NOPE), 1) < ROPE
            for pair in range(chunk_heads // 2):
                cols = slice(pair * 2 * NOPE, (pair + 1) * 2 * NOPE)
                w = wk[c, :, :, cols].reshape(rank, 2 * NOPE)
                k = jnp.dot(lat, w, preferred_element_type=jnp.float32)
                kaug[2 * pair, at, :NOPE] = k[:, :NOPE].astype(jnp.bfloat16)
                turned = pltpu.roll(k[:, NOPE:], ROPE, axis=1)
                zeros_first = jnp.where(low, 0.0, turned).astype(jnp.bfloat16)
                kaug[2 * pair + 1, at, :NOPE] = zeros_first
                rope_last = kaug[2 * pair + 1, at, NOPE:].astype(jnp.float32)
                kaug[2 * pair + 1, at, NOPE:] = jnp.where(low, turned, rope_last).astype(
                    jnp.bfloat16
                )
                w = wv[c, :, :, cols].reshape(rank, 2 * VDIM)
                v = jnp.dot(lat, w, preferred_element_type=jnp.float32)
                vbuf[at, cols] = v.astype(jnp.bfloat16)
            return carry

        lax.fori_loop(0, 2, rows_of, 0)

    scale = LOG2E / math.sqrt(QK)

    def attend(c, first_tile, last_tile):
        def tile(j, carry):
            at = pl.ds(pl.multiple_of(j * tok, tok), span)
            hide = bias[j]
            for h in range(chunk_heads):
                begin = (h // 2) * 2 * QK + (h % 2) * NOPE
                q = qbuf[c, j, :, begin:begin + 2 * NOPE]
                s = lax.dot_general(
                    q, kaug[h, at, :], (((1,), (1,)), ((), ())),
                    preferred_element_type=jnp.float32,
                )
                s = s * scale + hide
                peak = jnp.max(s, axis=1, keepdims=True)
                expo = jnp.exp2(s - peak)
                total = jnp.sum(expo, axis=1, keepdims=True)
                cols = slice(h * VDIM, (h + 1) * VDIM)
                mixed = jnp.dot(
                    expo.astype(jnp.bfloat16), vbuf[at, cols],
                    preferred_element_type=jnp.float32,
                )
                obuf[c, j, :, cols] = (mixed / total).astype(jnp.bfloat16)
            return carry

        lax.fori_loop(first_tile, last_tile, tile, 0)

    def q_in(c):
        for k in range(n_head):
            sender = (head + k) % n_head
            landed = qbuf.at[c, sender]
            pltpu.make_async_copy(landed, landed, q_sem.at[c, sender]).wait()

    def give(c):
        for k in range(1, n_head):
            o_copy(c, k).start()
        o_own(c).start()

    def work_on(c):
        middle = n_head // 2

        def tiles_first():
            q_in(c)
            attend(c, 0, middle)

        def tiles_last():
            attend(c, middle, n_head)
            give(c)

        return [functools.partial(project, c), tiles_first, tiles_last]

    waiting = []
    for base in range(0, chunks, 2):
        pair = range(base, min(base + 2, chunks))
        for t in range(1, half + 1):
            for c in pair:
                ring_take(c, t)
                if t == half - 1 and c == pair[-1]:
                    for ahead in range(base + 2, min(base + 4, chunks)):
                        ring_start(ahead, 1)
                if base == 0 and t == 1 and c == pair[-1]:
                    lat_all_in()
                    rope_in()
                if waiting:
                    waiting.pop(0)()
        for c in pair:
            waiting += work_on(c)
    for step in waiting:
        step()

    for c in range(chunks):
        for k in range(n_head):
            sender = (head + k) % n_head
            landed = out.at[:, pl.ds(pl.multiple_of(sender * chunks * cw + c * cw, 128), cw)]
            pltpu.make_async_copy(landed, landed, o_sem.at[c, sender]).wait()
        for k in range(1, n_head):
            q_copy(c, k).wait_send()
            o_copy(c, k).wait_send()
        for t in range(1, half + 1):
            for way, kv in ring_parts(t):
                ring_copy(c, t, way, kv).wait_send()
    for k in range(1, xs):
        lat_copy(k, seq, look + head).wait_send()

    @pl.when(head >= n_head - look)
    def _():
        for k in range(xs):
            lat_copy(xs + k, next_seq, head - (n_head - look)).wait_send()

    for i in range(slots // 2):
        mate_copy(i).wait_send()


def shards(queries, latent, rope_keys, key_weight, value_weight, doc_lengths):
    n_seq, n_head = lax.axis_size("seq"), lax.axis_size("head")
    tok, rank = latent.shape
    rows = key_weight.shape[0]
    local_heads = key_weight.shape[1] // NOPE
    docs = doc_lengths.shape[0]
    slot_rows = n_seq * n_head * tok // docs
    look = 2 * -(-slot_rows // tok)
    chunk_heads = min(4, local_heads)
    chunks = local_heads // chunk_heads
    slots, span, half = look + n_head, (look + 1) * tok, n_seq // 2
    cw, qw = chunk_heads * NOPE, chunk_heads * QK
    latrope = jnp.concatenate(
        [latent, rope_keys, jnp.zeros((tok, 2 * ROPE - rope_keys.shape[1]), latent.dtype)], axis=1
    )
    anywhere = pl.BlockSpec(memory_space=pl.ANY)
    dma = pltpu.SemaphoreType.DMA
    bf16 = jnp.bfloat16
    return pl.pallas_call(
        functools.partial(kernel, (n_seq, n_head, look, chunks, chunk_heads)),
        out_shape=jax.ShapeDtypeStruct((tok, n_head * local_heads * VDIM), bf16),
        in_specs=[anywhere] * 4 + [pl.BlockSpec(memory_space=pltpu.VMEM)],
        out_specs=anywhere,
        scratch_shapes=[
            pltpu.VMEM((slots, tok, rank + 2 * ROPE), bf16),
            pltpu.VMEM((chunks, n_seq, rows, cw), bf16),
            pltpu.VMEM((chunks, n_seq, rows, cw), bf16),
            pltpu.VMEM((chunks, n_head, tok, qw), bf16),
            pltpu.VMEM((chunk_heads, slots * tok, 2 * NOPE), bf16),
            pltpu.VMEM((slots * tok, cw), bf16),
            pltpu.VMEM((n_head, tok, span), jnp.float32),
            pltpu.VMEM((chunks, n_head, tok, cw), bf16),
            dma((slots,)),
            dma((n_head,)),
            dma((slots // 2,)),
            dma((chunks, n_head)),
            dma((chunks, n_head - 1)),
            dma((chunks, 2)),
            dma((chunks, half, 2, 2)),
            dma((chunks, half, 2, 2)),
            dma((chunks, n_head)),
            dma((chunks, n_head - 1)),
        ],
        compiler_params=pltpu.CompilerParams(collective_id=0, has_side_effects=True),
    )(queries, latrope, key_weight, value_weight, doc_lengths.reshape(docs, 1))


def solution(mesh):
    placed = (
        P(("seq", "head"), None),
        P(("seq", "head"), None),
        P(("seq", "head"), None),
        P("seq", "head"),
        P("seq", "head"),
        P(),
    )
    return jax.shard_map(
        shards, mesh=mesh, in_specs=placed, out_specs=P(("seq", "head"), None), check_vma=False
    )
```

time: 265 us -> 81.8 us (0.31)
  the two profiles are of different devices: /device:TPU:24 before, /device:TPU:1 now
where the time goes in v1:
time: 81.8 us; the launch traced here: 81.5 us
  Pallas kernels  74.5 us (91%)
  local copies, waits for them, and re-layouts  5.33 us (7%)
  other arithmetic  1.61 us (2%)
    pallas_call x1, Pallas kernels, shards(): pl.pallas_call(functools.partial(kernel, (n_seq, n_head, look, chunks, ch...  74.5 us
    unnamed x2, local copies, waits for them, and re-layouts  3.92 us

profile of v1, /device:TPU:1, one launch (start us, length us, event | category | flops | bytes accessed | tf_op | source)
XLA Modules:
  0.0 81.5 jit_solution(16499275804181504851)
XLA Ops:
  0.0 0.1 pad.2.clone
  0.1 1.3 %copy.8.lengths = s32[32,1]{1,0:T(8,128)} copy(s32[32,1]{0,1:T(1,128)} %bitcast.1) | data formatting | bytes 256 | tf_op jit(solution)/shard_map/reshape | solution.py:365
  1.4 0.8 %copy.7 = bf16[128,64]{1,0:T(8,128)(2,1)S(1)} copy(bf16[128,64]{0,1:T(8,128)(2,1)} %param.8) | data formatting | bytes 32768 | tf_op args[2]
  2.2 1.6 %maximum_maximum_fusion.latrope = bf16[128,640]{1,0:T(8,128)(2,1)} fusion(bf16[128,64]{1,0:T(8,128)(2,1)S(1)} %copy.7, bf16[128,512]{1,0:T(8,128)(2,1)} %param.7, bf16[640]{0:T(1024)(128)(2,1)S(1)} %pad.2.clone), kind=kLoop, calls=%fused_computation | loop fusion | flops 491520 | bytes 312576 | tf_op jit(solution)/shard_map/concatenate | solution.py:333
  3.9 74.5 %shard_map.64 = bf16[128,8192]{1,0:T(8,128)(2,1)} custom-call(bf16[128,12288]{1,0:T(8,128)(2,1)} %queries.1, bf16[128,640]{1,0:T(8,128)(2,1)} %maximum_maximum_fusion.latrope, bf16[64,2048]{1,0:T(8,128)(2,1)} %key_weight.1, bf16[64,2048]{1,0:T(8,128)(2,1)} %value_weight.1, s32[32,1]{1,0:T(8,128)} %copy.8.lengths), custom_call_target="tpu_custom_call" | custom-call | tf_op jit(solution)/shard_map/pallas_call | solution.py:339
  78.4 3.1 %copy.10 = bf16[128,8192]{1,0:T(8,128)(2,1)} copy(bf16[128,8192]{1,0:T(8,128)(2,1)} %shard_map.64) | data formatting | bytes 4194304
  (1 shorter events, 0.0 us)

commit v2 on v1

v2 whole, which is shorter than its diff:
```python
import functools
import math

import jax
import jax.numpy as jnp
from jax import lax
from jax.experimental import pallas as pl
from jax.experimental.pallas import tpu as pltpu
from jax.sharding import PartitionSpec as P

NOPE = 128
ROPE = 64
VDIM = 128
QK = NOPE + ROPE
LOG2E = 1.4426950408889634

MESH = pl.DeviceIdType.MESH


def kernel(
    sizes, queries, latent, rope_keys, key_weight, value_weight, lengths, out,
    lat_all, rope_all, wk, wv, qbuf, kaug, vbuf, bias, obuf,
    lat_sem, lat_send, mate_send, x_send, q_sem, q_send, w_own, w_recv, w_send, o_sem, o_send,
):
    n_seq, n_head, look, wide, chunk_heads = sizes
    tok, rank = latent.shape
    rows = key_weight.shape[0]
    half = n_seq // 2
    xs = n_head // 2
    slots = look + n_head
    span = (look + 1) * tok
    cw = chunk_heads * NOPE
    qw = chunk_heads * QK
    pieces = wide + xs
    q_all, o_all = (wide + 1) * qw, (wide + 1) * cw
    seq, head = lax.axis_index("seq"), lax.axis_index("head")
    core, x = head % 2, head // 2
    mate = head + 1 - 2 * core

    odd = seq % 2
    place = (seq // 2) * (1 - odd) + (n_seq - 1 - seq // 2) * odd

    def at_place(where):
        where = (where + n_seq) % n_seq
        fold = where // half
        return 2 * where * (1 - fold) + (2 * (n_seq - 1 - where) + 1) * fold

    after, before = at_place(place + 1), at_place(place - 1)
    next_seq, last_seq = (seq + 1) % n_seq, (seq + n_seq - 1) % n_seq

    barrier = pltpu.get_barrier_semaphore()

    def greet(to_seq, to_head):
        pl.semaphore_signal(barrier, inc=1, device_id=(to_seq, to_head), device_id_type=MESH)

    for k in range(1, n_head):
        greet(seq, (head + k) % n_head)
    greet(after, head)
    greet(before, head)
    for k in range(xs):
        greet(next_seq, ((x + k) % xs) * 2 + core)
        greet(last_seq, ((x + k) % xs) * 2 + core)

    def owner(k, side):
        return ((x + k) % xs) * 2 + side

    def q_cols(who, c):
        return pl.ds(pl.multiple_of(who * q_all + c * qw, 128), qw)

    def o_cols(who, c):
        return pl.ds(pl.multiple_of(who * o_all + c * cw, 128), cw)

    def own_copies():
        mine = look + head
        pltpu.make_async_copy(latent, lat_all.at[mine], lat_sem.at[mine, 0]).start()
        pltpu.make_async_copy(rope_keys, rope_all.at[mine], lat_sem.at[mine, 1]).start()
        for c in range(wide + 1):
            for kv, (source, held) in enumerate(((key_weight, wk), (value_weight, wv))):
                pltpu.make_async_copy(
                    source.at[:, pl.ds(c * cw, cw)], held.at[c, seq], w_own.at[c, kv]
                ).start()
        for c in range(wide):
            pltpu.make_async_copy(
                queries.at[:, q_cols(head, c)], qbuf.at[c, head], q_sem.at[c, head]
            ).start()
        for k in range(xs):
            pltpu.make_async_copy(
                queries.at[:, q_cols(owner(k, core), wide)],
                qbuf.at[wide + k, core], q_sem.at[wide + k, core],
            ).start()

    own_copies()
    pl.semaphore_wait(barrier, n_head - 1 + 2 + 2 * xs)

    def lat_copies(k, to_seq, slot):
        return [
            pltpu.make_async_remote_copy(
                src_ref=source, dst_ref=held.at[slot],
                send_sem=lat_send.at[k, part], recv_sem=lat_sem.at[slot, part],
                device_id=(to_seq, ((x + k % xs) % xs) * 2 + core), device_id_type=MESH,
            )
            for part, (source, held) in enumerate(((latent, lat_all), (rope_keys, rope_all)))
        ]

    def x_copies(k):
        return [
            pltpu.make_async_remote_copy(
                src_ref=source.at[:, pl.ds(wide * cw, cw)], dst_ref=held.at[wide + k, seq],
                send_sem=x_send.at[k - 1, kv], recv_sem=w_own.at[wide + k, kv],
                device_id=(seq, ((x + xs - k) % xs) * 2 + core), device_id_type=MESH,
            )
            for kv, (source, held) in enumerate(((key_weight, wk), (value_weight, wv)))
        ]

    def ring_parts(t):
        both = [(0, 0), (0, 1), (1, 0), (1, 1)]
        return both if t < half else [(0, 0), (1, 1)]

    def own_weights(c):
        for kv in range(2):
            mine = (wk, wv)[kv].at[c, seq]
            pltpu.make_async_copy(mine, mine, w_own.at[c, kv]).wait()

    def ring_copy(c, t, way, kv):
        origin = at_place(place - (t - 1)) if way == 0 else at_place(place + (t - 1))
        source, held = ((key_weight, wk), (value_weight, wv))[kv]
        src = source.at[:, pl.ds(c * cw, cw)] if t == 1 and c <= wide else held.at[c, origin]
        index = t - 1
        return pltpu.make_async_remote_copy(
            src_ref=src, dst_ref=held.at[c, origin],
            send_sem=w_send.at[c, index, way, kv], recv_sem=w_recv.at[c, index, way, kv],
            device_id=(after if way == 0 else before, head), device_id_type=MESH,
        )

    def ring_start(c, t):
        if c > wide:
            own_weights(c)
        for way, kv in ring_parts(t):
            ring_copy(c, t, way, kv).start()

    def ring_take(c, t):
        for way, kv in ring_parts(t):
            origin = at_place(place - t) if way == 0 else at_place(place + t)
            landed = (wk, wv)[kv].at[c, origin]
            pltpu.make_async_copy(landed, landed, w_recv.at[c, t - 1, way, kv]).wait()
            if t + 1 <= half and (way, kv) in ring_parts(t + 1):
                ring_copy(c, t + 1, way, kv).start()

    def q_copies(c):
        if c < wide:
            routes = [((head + k) % n_head,) * 2 + (head,) for k in range(1, n_head)]
        else:
            routes = [(mate, owner(c - wide, 1 - core), core)]
        return [
            pltpu.make_async_remote_copy(
                src_ref=queries.at[:, q_cols(who, min(c, wide))], dst_ref=qbuf.at[c, slot],
                send_sem=q_send.at[c, k], recv_sem=q_sem.at[c, slot],
                device_id=(seq, peer), device_id_type=MESH,
            )
            for k, (peer, who, slot) in enumerate(routes)
        ]

    def o_copies(c):
        if c < wide:
            routes = [((head + k) % n_head,) * 2 + (head, head) for k in range(1, n_head)]
        else:
            routes = [(mate, 1 - core, owner(c - wide, core), core)]
        return [
            pltpu.make_async_remote_copy(
                src_ref=obuf.at[c, tile], dst_ref=out.at[:, o_cols(who, min(c, wide))],
                send_sem=o_send.at[c, k], recv_sem=o_sem.at[c, slot],
                device_id=(seq, peer), device_id_type=MESH,
            )
            for k, (peer, tile, who, slot) in enumerate(routes)
        ]

    def o_own(c):
        if c < wide:
            tile, who, slot = head, head, head
        else:
            tile, who, slot = core, owner(c - wide, core), core
        return pltpu.make_async_copy(
            obuf.at[c, tile], out.at[:, o_cols(who, min(c, wide))], o_sem.at[c, slot]
        )

    for k in range(1, xs):
        for copy in lat_copies(k, seq, look + head):
            copy.start()

    @pl.when(head >= n_head - look)
    def _():
        for k in range(xs):
            for copy in lat_copies(xs + k, next_seq, head - (n_head - look)):
                copy.start()

    groups = [list(range(wide)), list(range(wide, pieces))]
    for c in groups[0]:
        ring_start(c, 1)
    for c in range(pieces):
        for copy in q_copies(c):
            copy.start()
        if c == 0:
            for k in range(1, xs):
                for copy in x_copies(k):
                    copy.start()

    docs = lengths.shape[0]
    first = seq * n_head * tok

    def mask_tile(j, carry):
        q_place = first + j * tok + lax.broadcasted_iota(jnp.int32, (tok, 1), 0)

        def document(d, state):
            start, begun = state
            return start + lengths[d], jnp.where(start <= q_place, start, begun)

        _, begun = lax.fori_loop(
            0, docs, document, (jnp.int32(0), jnp.zeros((tok, 1), jnp.int32)), unroll=True
        )
        k_place = first + (j - look) * tok + lax.broadcasted_iota(jnp.int32, (tok, span), 1)
        seen = (k_place >= begun) & (k_place <= q_place)
        bias[j] = jnp.where(seen, 0.0, -jnp.inf)
        return carry

    lax.fori_loop(0, n_head, mask_tile, 0)

    def lat_wait(slot):
        for part, held in enumerate((lat_all, rope_all)):
            pltpu.make_async_copy(held.at[slot], held.at[slot], lat_sem.at[slot, part]).wait()

    def mate_copies(i):
        slot = 2 * i + core
        return [
            pltpu.make_async_remote_copy(
                src_ref=held.at[slot], dst_ref=held.at[slot],
                send_sem=mate_send.at[i, part], recv_sem=lat_sem.at[slot, part],
                device_id=(seq, mate), device_id_type=MESH,
            )
            for part, held in enumerate((lat_all, rope_all))
        ]

    def lat_all_in():
        for i in list(range(look // 2, slots // 2)) + list(range(look // 2)):
            lat_wait(2 * i + core)
            for copy in mate_copies(i):
                copy.start()
        for i in range(slots // 2):
            lat_wait(2 * i + 1 - core)

    def rope_in():
        first_half = lax.broadcasted_iota(jnp.int32, (tok, 2 * ROPE), 1) < ROPE

        def fill(slot, carry):
            rope = rope_all[slot].astype(jnp.float32)
            twice = jnp.concatenate([rope, rope], axis=1)
            at = pl.ds(pl.multiple_of(slot * tok, tok), tok)
            for h in range(chunk_heads):
                shown = jnp.where(first_half, twice, 0.0) if h % 2 == 0 else twice
                kaug[h, at, NOPE:] = shown.astype(jnp.bfloat16)
            return carry

        lax.fori_loop(0, slots, fill, 0)

    block = 2 * tok

    def project(c):
        if c <= wide:
            own_weights(c)
        first_slot, blocks = (0, slots // 2) if c < wide else (2 * x, (look + 2) // 2)

        def rows_of(i, carry):
            slot = first_slot + 2 * i
            at = pl.ds(pl.multiple_of(slot * tok, tok), block)
            lat = lat_all[pl.ds(slot, 2)].reshape(block, rank)
            low = lax.broadcasted_iota(jnp.int32, (block, NOPE), 1) < ROPE
            for pair in range(chunk_heads // 2):
                cols = slice(pair * 2 * NOPE, (pair + 1) * 2 * NOPE)
                w = wk[c, :, :, cols].reshape(rank, 2 * NOPE)
                k = jnp.dot(lat, w, preferred_element_type=jnp.float32)
                kaug[2 * pair, at, :NOPE] = k[:, :NOPE].astype(jnp.bfloat16)
                turned = pltpu.roll(k[:, NOPE:], ROPE, axis=1)
                zeros_first = jnp.where(low, 0.0, turned).astype(jnp.bfloat16)
                kaug[2 * pair + 1, at, :NOPE] = zeros_first
                rope_last = kaug[2 * pair + 1, at, NOPE:].astype(jnp.float32)
                kaug[2 * pair + 1, at, NOPE:] = jnp.where(low, turned, rope_last).astype(
                    jnp.bfloat16
                )
                w = wv[c, :, :, cols].reshape(rank, 2 * VDIM)
                v = jnp.dot(lat, w, preferred_element_type=jnp.float32)
                vbuf[at, cols] = v.astype(jnp.bfloat16)
            return carry

        lax.fori_loop(0, blocks, rows_of, 0)

    scale = LOG2E / math.sqrt(QK)

    def attend(c, first_tile, last_tile):
        def tile(j, carry):
            place_of = j if c < wide else 2 * x + j
            at = pl.ds(pl.multiple_of(place_of * tok, tok), span)
            hide = bias[place_of]
            for h in range(chunk_heads):
                begin = (h // 2) * 2 * QK + (h % 2) * NOPE
                q = qbuf[c, j, :, begin:begin + 2 * NOPE]
                s = lax.dot_general(
                    q, kaug[h, at, :], (((1,), (1,)), ((), ())),
                    preferred_element_type=jnp.float32,
                )
                s = s * scale + hide
                peak = jnp.max(s, axis=1, keepdims=True)
                expo = jnp.exp2(s - peak)
                total = jnp.sum(expo, axis=1, keepdims=True)
                cols = slice(h * VDIM, (h + 1) * VDIM)
                mixed = jnp.dot(
                    expo.astype(jnp.bfloat16), vbuf[at, cols],
                    preferred_element_type=jnp.float32,
                )
                obuf[c, j, :, cols] = (mixed / total).astype(jnp.bfloat16)
            return carry

        lax.fori_loop(first_tile, last_tile, tile, 0)

    def q_in(c):
        for slot in range(n_head if c < wide else 2):
            landed = qbuf.at[c, slot]
            pltpu.make_async_copy(landed, landed, q_sem.at[c, slot]).wait()

    def give(c):
        for copy in o_copies(c):
            copy.start()
        o_own(c).start()

    def work_on(c):
        tiles = n_head if c < wide else 2

        def tiles_first():
            q_in(c)
            attend(c, 0, tiles // 2)

        def tiles_last():
            attend(c, tiles // 2, tiles)
            give(c)

        return [functools.partial(project, c), tiles_first, tiles_last]

    waiting = []
    for number, group in enumerate(groups):
        for t in range(1, half + 1):
            for c in group:
                ring_take(c, t)
                if t == half - 1 and c == group[-1] and number + 1 < len(groups):
                    for ahead in groups[number + 1]:
                        ring_start(ahead, 1)
                if number == 0 and t == 1 and c == group[-1]:
                    lat_all_in()
                    rope_in()
                if t == half:
                    waiting += work_on(c)
                for _ in range(min(1, len(waiting))):
                    waiting.pop(0)()
    for step in waiting:
        step()

    for c in range(pieces):
        for slot in range(n_head if c < wide else 2):
            who = slot if c < wide else owner(c - wide, slot)
            landed = out.at[:, o_cols(who, min(c, wide))]
            pltpu.make_async_copy(landed, landed, o_sem.at[c, slot]).wait()
        for copy in q_copies(c) + o_copies(c):
            copy.wait_send()
        for t in range(1, half + 1):
            for way, kv in ring_parts(t):
                ring_copy(c, t, way, kv).wait_send()
    for k in range(1, xs):
        for copy in lat_copies(k, seq, look + head) + x_copies(k):
            copy.wait_send()

    @pl.when(head >= n_head - look)
    def _():
        for k in range(xs):
            for copy in lat_copies(xs + k, next_seq, head - (n_head - look)):
                copy.wait_send()

    for i in range(slots // 2):
        for copy in mate_copies(i):
            copy.wait_send()


def shards(queries, latent, rope_keys, key_weight, value_weight, doc_lengths):
    n_seq, n_head = lax.axis_size("seq"), lax.axis_size("head")
    tok, rank = latent.shape
    rows = key_weight.shape[0]
    local_heads = key_weight.shape[1] // NOPE
    docs = doc_lengths.shape[0]
    slot_rows = n_seq * n_head * tok // docs
    look = 2 * -(-slot_rows // tok)
    chunk_heads = min(4, local_heads)
    wide = local_heads // chunk_heads - 1
    pieces = wide + n_head // 2
    slots, span, half = look + n_head, (look + 1) * tok, n_seq // 2
    cw, qw = chunk_heads * NOPE, chunk_heads * QK
    anywhere = pl.BlockSpec(memory_space=pl.ANY)
    dma = pltpu.SemaphoreType.DMA
    bf16 = jnp.bfloat16
    return pl.pallas_call(
        functools.partial(kernel, (n_seq, n_head, look, wide, chunk_heads)),
        out_shape=jax.ShapeDtypeStruct((tok, n_head * local_heads * VDIM), bf16),
        in_specs=[anywhere] * 5 + [pl.BlockSpec(memory_space=pltpu.SMEM)],
        out_specs=anywhere,
        scratch_shapes=[
            pltpu.VMEM((slots, tok, rank), bf16),
            pltpu.VMEM((slots, tok, ROPE), bf16),
            pltpu.VMEM((pieces, n_seq, rows, cw), bf16),
            pltpu.VMEM((pieces, n_seq, rows, cw), bf16),
            pltpu.VMEM((pieces, n_head, tok, qw), bf16),
            pltpu.VMEM((chunk_heads, slots * tok, 2 * NOPE), bf16),
            pltpu.VMEM((slots * tok, cw), bf16),
            pltpu.VMEM((n_head, tok, span), jnp.float32),
            pltpu.VMEM((pieces, n_head, tok, cw), bf16),
            dma((slots, 2)),
            dma((n_head, 2)),
            dma((slots // 2, 2)),
            dma((n_head // 2 - 1, 2)),
            dma((pieces, n_head)),
            dma((pieces, n_head - 1)),
            dma((pieces, 2)),
            dma((pieces, half, 2, 2)),
            dma((pieces, half, 2, 2)),
            dma((pieces, n_head)),
            dma((pieces, n_head - 1)),
        ],
        compiler_params=pltpu.CompilerParams(collective_id=0, has_side_effects=True),
    )(queries, latent, rope_keys, key_weight, value_weight, doc_lengths)


def solution(mesh):
    placed = (
        P(("seq", "head"), None),
        P(("seq", "head"), None),
        P(("seq", "head"), None),
        P("seq", "head"),
        P("seq", "head"),
        P(),
    )
    return jax.shard_map(
        shards, mesh=mesh, in_specs=placed, out_specs=P(("seq", "head"), None), check_vma=False
    )
```

time: 81.8 us -> 78 us (0.954)
  Pallas kernels: 74.5 us -> 72.8 us
  other arithmetic: 1.61 us -> 0 us
    pallas_call x1, Pallas kernels: 74.5 us -> 72.8 us  [shards(): pl.pallas_call(functools.partial(kernel, (n_seq, n_head, look, wide, chun...]
    concatenate x1 -> x0, other arithmetic: 1.61 us -> none  [shards(): jnp.concatenate([latent, rope_keys, jnp.zeros((tok, 2 * ROPE - rope_keys....]
    reshape x1 -> x0, local copies, waits for them, and re-layouts: 1.33 us -> none  [shards(): doc_lengths.reshape(docs, 1)]
where the time goes in v2:
time: 78 us; the launch traced here: 77.3 us
  Pallas kernels  72.8 us (93%)
  local copies, waits for them, and re-layouts  4.53 us (6%)
    pallas_call x1, Pallas kernels, shards(): pl.pallas_call(functools.partial(kernel, (n_seq, n_head, look, wide, chun...  72.8 us
    unnamed x2, local copies, waits for them, and re-layouts  4.53 us

profile of v2, /device:TPU:1, one launch (start us, length us, event | category | flops | bytes accessed | tf_op | source)
XLA Modules:
  0.0 77.3 jit_solution(13779632904228752247)
XLA Ops:
  0.0 1.4 %copy.7.rope_keys = bf16[128,64]{1,0:T(8,128)(2,1)} copy(bf16[128,64]{0,1:T(8,128)(2,1)} %param.8) | data formatting | bytes 32768 | tf_op args[2]
  1.4 72.8 %shard_map.64 = bf16[128,8192]{1,0:T(8,128)(2,1)} custom-call(bf16[128,12288]{1,0:T(8,128)(2,1)} %queries.1, bf16[128,512]{1,0:T(8,128)(2,1)} %latent.1, bf16[128,64]{1,0:T(8,128)(2,1)} %copy.7.rope_keys, bf16[64,2048]{1,0:T(8,128)(2,1)} %key_weight.1, bf16[64,2048]{1,0:T(8,128)(2,1)} %value_weight.1, s32[32]{0:T(128)} %lengths.1), custom_call_target="tpu_custom_call" | custom-call | tf_op jit(solution)/shard_map/pallas_call | solution.py:405
  74.2 3.1 %copy.9 = bf16[128,8192]{1,0:T(8,128)(2,1)} copy(bf16[128,8192]{1,0:T(8,128)(2,1)} %shard_map.64) | data formatting | bytes 4194304
